TPU v7x, 512 devices: a whole 4x8x8 slice. The times are simulated.
512 devices in a mesh: tm: 256 (over x, z, y), det: 2 (over core).
Axes of the slice: x: 4, y: 8, z: 8, core: 2. Of those that a mesh axis runs over, the one named last changes fastest.
Arguments:
- strain: float32 [2, 1024, 192, 512], P('det', 'tm'), may hold values from -24 to 24
- final_half: float32 [2, 192, 512], P('det'), may hold values from -6 to 6
- intersection_function: float32 [16384], P('det'), may hold values from -1 to 1
- notch_mask: int32 [16384], P('det'), may hold values 0 or 1
- quality_flags: int32 [1024], P('tm'), may hold values 0 or 1
Outputs:
- csd: float32 [1024, 2, 16384], P('tm', None, 'det')
- stats: float32 [3, 1024], P(None, 'tm')
- combined: float32 [2], replicated
All inputs are finite; a program needn't handle non-finite values. No bound on the sum of `notch_mask` or of `quality_flags` on one device may be relied on, other than what follows from the above.
Results may differ from a plain program's by a relative error of at most 0.0003.
Values sent between devices are 32-bit elements; how exact they have to be, the bound alone decides.
A program may use at most 64 MiB of HBM per device.

v0:
```python
import functools

import jax
import jax.numpy as jnp
import numpy as np
from jax import lax
from jax.experimental import pallas as pl
from jax.experimental.pallas import tpu as pltpu
from jax.sharding import PartitionSpec as P

MESH = pl.DeviceIdType.MESH
F32 = jnp.float32
BF16 = jnp.bfloat16

HALF = 192
FULL = 384
COLS = 512
LENGTH = FULL * COLS
KBLK = 256
BIN = 6
GROUPS = FULL // BIN
COARSE = 16384
KPAD = 256
CORR = 27.0 / 154.0
SEG = 4


def split_np(table):
    high = table.astype(np.float32).astype(BF16)
    low = (table - high.astype(np.float64)).astype(np.float32).astype(BF16)
    return high, low


@functools.cache
def tables():
    row = np.arange(HALF)
    col = np.arange(COLS)
    window = np.sin(np.pi * (row[:, None] * COLS + col[None, :]) / LENGTH) ** 2

    ones, twists = [], []
    for parity in range(2):
        bins = np.concatenate([BIN * np.arange(GROUPS) + r for r in range(parity, BIN, 2)])
        angle = 2.0 * np.pi * (bins[:, None] * row[None, :] % FULL) / FULL
        one = np.concatenate([np.cos(angle), -np.sin(angle)], axis=0)
        ones.append(np.pad(one, ((0, 0), (0, KPAD - HALF))))
        turn = 2.0 * np.pi * (bins[:, None] * col[None, :] % LENGTH) / LENGTH
        twists.append(np.stack([np.cos(turn), np.sin(turn)]))
    one_hi, one_lo = split_np(np.stack(ones))

    twos = []
    for q in range(2):
        parts = []
        for band in range(2):
            k2 = 2 * (64 * band + np.arange(64)) + q
            angle = 2.0 * np.pi * (np.arange(256)[:, None] * k2[None, :] % COLS) / COLS
            c, s = np.cos(angle), np.sin(angle)
            parts.append(np.concatenate([c, s], axis=0))
            parts.append(np.concatenate([-s, c], axis=0))
        twos.append(np.concatenate(parts, axis=1))
    two_hi, two_lo = split_np(np.stack(twos) * (8.0 / (3.0 * LENGTH) / BIN) ** 0.5)
    return (
        window.astype(np.float32),
        np.stack([one_hi, one_lo], axis=1),
        np.stack(twists).astype(np.float32),
        np.stack([two_hi, two_lo], axis=1),
    )


def kernel(
    dims,
    strain, final, func, mask, flags, window, ones, twist, twos,
    csd, stats, combined,
    h, win, one, twi, two, fnat, mnat, rhs, y, lhs, xb, rb, pw, pn, pp, ob, sums, rsums, gath, flag, rflag, fg, re_c,
    load_sem, half_send, half_recv, x_send, x_recv, p_send, p_recv, s_sem, g_send, g_recv, o_sem,
):
    nx, nz, ny = dims
    total = nx * nz * ny
    me = lax.axis_index("tm")
    det = lax.axis_index("det")
    cy = lax.rem(me, ny)
    cz = lax.rem(me // ny, nz)
    cx = me // (ny * nz)
    prev = lax.rem(me + total - 1, total)
    following = lax.rem(me + 1, total)
    first = me == 0
    last = me == total - 1

    def y_peer(k):
        return (cx * nz + cz) * ny + k

    def z_peer(k):
        return (cx * nz + k) * ny + cy

    def x_peer(k):
        return (k * nz + cz) * ny + cy

    axes = ((ny, cy, y_peer), (nz, cz, z_peer), (nx, cx, x_peer))

    barrier = pltpu.get_barrier_semaphore()
    peers = [(prev, det), (following, det), (me, 1 - det)]
    for count, mine, peer in axes:
        for d in range(1, count):
            peers.append((peer(lax.rem(mine + d, count)), det))
    for peer in peers:
        pl.semaphore_signal(barrier, inc=1, device_id=peer, device_id_type=MESH)

    loads = []

    def load(src, dst):
        copy = pltpu.make_async_copy(src, dst, load_sem.at[len(loads)])
        copy.start()
        loads.append(copy)

    load(window, win)
    for s in range(SEG):
        load(strain.at[0, s], h.at[s])
    for parity in range(2):
        for part in range(3):
            load(ones.at[parity, part % 2], one.at[parity, :, pl.ds(KPAD * part, KPAD)])
    load(twist, twi)
    for q in range(2):
        for part in range(3):
            load(twos.at[q, (0, 0, 1)[part]], two.at[q, pl.ds(512 * part, 512)])
    load(func, fnat)
    load(mask, mnat)

    flag[...] = jnp.full((8, 128), flags[0].astype(F32), F32)
    gap = jnp.zeros((KPAD - HALF, COLS), BF16)
    for parity in range(2):
        for part in range(3):
            rhs[parity, pl.ds(KPAD * part + HALF, KPAD - HALF), :] = gap
    sums[...] = jnp.zeros((16, 128), F32)

    pl.semaphore_wait(barrier, len(peers))

    def half_copy(p):
        cols = pl.ds(256 * p, 256)
        return pltpu.make_async_remote_copy(
            src_ref=strain.at[0, 0, :, cols],
            dst_ref=h.at[SEG, :, cols],
            send_sem=half_send.at[p],
            recv_sem=half_recv.at[p],
            device_id=(prev, det),
            device_id_type=MESH,
        )

    @pl.when(jnp.logical_not(first))
    def _():
        for p in range(2):
            half_copy(p).start()

    def flag_copy():
        return pltpu.make_async_remote_copy(
            src_ref=flag, dst_ref=rflag, send_sem=p_send.at[3], recv_sem=p_recv.at[3],
            device_id=(prev, det), device_id_type=MESH,
        )

    flag_copy().start()

    def last_copy():
        return pltpu.make_async_copy(final.at[0], h.at[SEG], o_sem.at[SEG])

    @pl.when(last)
    def _():
        last_copy().start()

    for copy in loads:
        copy.wait()

    low_lane = lax.broadcasted_iota(jnp.int32, (64, 128), 1) < 64

    f_nat = fnat[...]
    g_nat = f_nat * mnat[...].astype(F32)
    fg[...] = jnp.concatenate(
        [
            jnp.where(low_lane, f_nat, pltpu.roll(g_nat, 64, 1)),
            jnp.where(low_lane, pltpu.roll(f_nat, 64, 1), g_nat),
        ],
        axis=0,
    ).T

    def split(value):
        high = value.astype(BF16)
        return high, (value - high.astype(F32)).astype(BF16)

    def transform(s, arriving):
        for p in range(2):
            cols = pl.ds(256 * p, 256)
            if arriving:

                @pl.when(jnp.logical_not(last))
                def _():
                    half_copy(p).wait_recv()

                if p == 0:

                    @pl.when(last)
                    def _():
                        last_copy().wait()

            def windowed(i, carry):
                rows = pl.ds(pl.multiple_of(16 * i, 16), 16)
                upper = h[s, rows, cols]
                lower = h[s + 1, rows, cols]
                w = win[rows, cols]
                for parity, value in ((0, lower + w * (upper - lower)), (1, w * (upper + lower) - lower)):
                    high, low = split(value)
                    rhs[parity, rows, cols] = high
                    rhs[parity, pl.ds(pl.multiple_of(KPAD + 16 * i, 16), 16), cols] = high
                    rhs[parity, pl.ds(pl.multiple_of(2 * KPAD + 16 * i, 16), 16), cols] = low
                return carry

            lax.fori_loop(0, HALF // 16, windowed, 0)
            for parity in range(2):
                y[parity, :, cols] = jnp.dot(one[parity], rhs[parity, :, cols], preferred_element_type=F32)

        def turned(i, carry):
            rows = pl.ds(pl.multiple_of(16 * i, 16), 16)
            for parity in range(2):
                real = y[parity, rows, :]
                imag = y[parity, pl.ds(pl.multiple_of(HALF + 16 * i, 16), 16), :]
                c = twi[parity, 0, rows, :]
                n = twi[parity, 1, rows, :]
                zr = real * c + imag * n
                zi = imag * c - real * n
                out_rows = pl.ds(pl.multiple_of(HALF * parity + 16 * i, 16), 16)
                for q in range(2):
                    for at, z in ((0, zr), (256, zi)):
                        high, low = split(z[:, :256] + z[:, 256:] if q == 0 else z[:, :256] - z[:, 256:])
                        lhs[q, out_rows, pl.ds(at, 256)] = high
                        lhs[q, out_rows, pl.ds(512 + at, 256)] = low
                        lhs[q, out_rows, pl.ds(1024 + at, 256)] = high
            return carry

        lax.fori_loop(0, HALF // 16, turned, 0)
        for q in range(2):
            out = jnp.dot(lhs[q], two[q], preferred_element_type=F32)
            xb[s, q, 0] = out[:, :128]
            xb[s, q, 1] = out[:, 128:]
            x_copy(s, q).start()

    def x_copy(s, q):
        return pltpu.make_async_remote_copy(
            src_ref=xb.at[s, q, 1 - det], dst_ref=rb.at[s, q], send_sem=x_send.at[s, q], recv_sem=x_recv.at[s, q],
            device_id=(me, 1 - det), device_id_type=MESH,
        )

    sign = 1.0 - 2.0 * det.astype(F32)

    def crossed(s):
        parts = []
        for q in range(2):
            x_copy(s, q).wait_recv()
            same = jnp.zeros((64, 128), F32)
            swap = jnp.zeros((64, 128), F32)
            power_a = jnp.zeros((64, 128), F32)
            power_b = jnp.zeros((64, 128), F32)
            for r in range(BIN):
                rows = pl.ds(64 * r, 64)
                a = xb[s, q, det, rows, :]
                b = rb[s, q, rows, :]
                same = same + a * b
                swap = swap + a * pltpu.roll(b, 64, 1)
                power_a = power_a + a * a
                power_b = power_b + b * b
            parts.append(
                (
                    same + pltpu.roll(same, 64, 1),
                    swap - pltpu.roll(swap, 64, 1),
                    power_a + pltpu.roll(power_a, 64, 1),
                    power_b + pltpu.roll(power_b, 64, 1),
                )
            )
        even, odd = parts
        real = jnp.where(low_lane, even[0], odd[0])
        imag = jnp.where(low_lane, even[1], -odd[1]) * sign
        pw[s, 0] = jnp.where(low_lane, even[2], odd[2])
        pw[s, 1] = jnp.where(low_lane, even[3], odd[3])
        re_c[s] = real
        turned = jnp.concatenate([real, imag], axis=0).T
        top, bottom = turned[:64], turned[64:]
        ob[s, pl.ds(0, 64, stride=2), :] = jnp.where(low_lane, top, pltpu.roll(bottom, 64, 1))
        ob[s, pl.ds(1, 64, stride=2), :] = jnp.where(low_lane, pltpu.roll(top, 64, 1), bottom)
        out_copy(s).start()

    def out_copy(s):
        return pltpu.make_async_copy(ob.at[s], csd.at[s], o_sem.at[s])

    def power_copy(which):
        if which < 2:
            return pltpu.make_async_remote_copy(
                src_ref=pw.at[which], dst_ref=pn.at[which], send_sem=p_send.at[which], recv_sem=p_recv.at[which],
                device_id=(prev, det), device_id_type=MESH,
            )
        return pltpu.make_async_remote_copy(
            src_ref=pw.at[SEG - 1], dst_ref=pp, send_sem=p_send.at[2], recv_sem=p_recv.at[2],
            device_id=(following, det), device_id_type=MESH,
        )

    transform(0, False)
    transform(1, False)
    crossed(0)
    power_copy(0).start()
    transform(2, False)
    crossed(1)
    power_copy(1).start()
    crossed(2)
    transform(3, True)
    crossed(3)
    power_copy(2).start()

    f_t = fg[pl.ds(0, 64), :]
    g_t = fg[pl.ds(64, 64), :]

    def accumulate(s, left, right, weight_left, weight_right):
        mean_a = left(0) * weight_left + right(0) * weight_right
        mean_b = left(1) * weight_left + right(1) * weight_right
        filt = g_t / (mean_a * mean_b)
        if s < SEG:
            sums[pl.ds(s, 1), :] = jnp.sum(filt * re_c[s], axis=0, keepdims=True)
        sums[pl.ds(8 + s, 1), :] = jnp.sum(filt * f_t, axis=0, keepdims=True)

    def own(s):
        return lambda a: pw[s, a]

    def ahead(s):
        return lambda a: pn[s, a]

    for s in (1, 2):
        accumulate(s, own(s - 1), own(s + 1), 0.5, 0.5)
    power_copy(0).wait_recv()
    ends = jnp.where(last, 1.0, 0.5).astype(F32)
    accumulate(3, own(2), ahead(0), ends, 1.0 - ends)
    power_copy(1).wait_recv()
    accumulate(4, own(3), ahead(1), 0.5, 0.5)
    power_copy(2).wait_recv()
    starts = jnp.where(first, 1.0, 0.5).astype(F32)
    accumulate(0, lambda a: pp[a], own(1), 1.0 - starts, starts)

    sum_copy = pltpu.make_async_remote_copy(
        src_ref=sums, dst_ref=rsums, send_sem=s_sem.at[0], recv_sem=s_sem.at[1],
        device_id=(me, 1 - det), device_id_type=MESH,
    )
    sum_copy.start()
    flag_copy().wait_recv()
    lane = lax.broadcasted_iota(jnp.int32, (8, 128), 1)
    row = lax.broadcasted_iota(jnp.int32, (8, 128), 0)
    quality = jnp.zeros((8, 128), F32)
    for s in range(SEG):
        quality = jnp.where(lane == s, flags[s].astype(F32), quality)
    quality = jnp.where(lane == SEG, rflag[...], quality)
    sum_copy.wait_recv()
    whole = jnp.sum(sums[...] + rsums[...], axis=1, keepdims=True)

    def to_lanes(column):
        spread_out = jnp.where(lane == row, jnp.broadcast_to(column, (8, 128)), 0.0)
        return jnp.broadcast_to(jnp.sum(spread_out, axis=0, keepdims=True), (8, 128))

    numerator = to_lanes(whole[:8])
    denominator = to_lanes(whole[8:])
    spread = jnp.sqrt(float(COARSE) / denominator)
    estimate = float(np.sqrt(12.0 * COARSE)) * numerator / denominator
    next_spread = pltpu.roll(spread, 127, 1)
    next_quality = pltpu.roll(quality, 127, 1)
    no_next = jnp.logical_and(lane == SEG - 1, last)
    up_next = jnp.where(no_next, 0.0, next_quality * next_spread)
    down_next = jnp.where(no_next, 0.0, next_quality / next_spread)
    covariance = CORR * quality * spread * up_next
    pair_term = CORR * quality / spread * down_next
    weight = quality / (spread * spread)
    rows3 = jnp.where(row == 0, estimate, jnp.where(row == 1, spread, covariance))
    stats[...] = rows3[:3, :SEG]
    terms = jnp.where(row == 0, weight, jnp.where(row == 1, weight * estimate, pair_term))
    terms = jnp.where(jnp.logical_and(lane < SEG, row < 3), terms, 0.0)

    for axis, (count, mine, peer) in enumerate(axes):
        gath[axis, mine] = terms

        def gather_copy(d, axis=axis, count=count, mine=mine, peer=peer):
            return pltpu.make_async_remote_copy(
                src_ref=gath.at[axis, mine], dst_ref=gath.at[axis, mine],
                send_sem=g_send.at[axis, d], recv_sem=g_recv.at[axis, mine],
                device_id=(peer(lax.rem(mine + d, count)), det), device_id_type=MESH,
            )

        for d in range(1, count):
            gather_copy(d).start()
        for d in range(1, count):
            source = lax.rem(mine + d, count)
            pltpu.make_async_remote_copy(
                src_ref=gath.at[axis, source], dst_ref=gath.at[axis, source],
                send_sem=g_send.at[axis, d], recv_sem=g_recv.at[axis, source],
                device_id=(peer(source), det), device_id_type=MESH,
            ).wait_recv()
        terms = gath[axis, 0]
        for k in range(1, count):
            terms = terms + gath[axis, k]

    sweep = jnp.sum(terms, axis=1, keepdims=True)
    weight_sum, weighted_sum, pair_sum = sweep[0:1], sweep[1:2], sweep[2:3]
    root = float(np.sqrt(SEG * total))
    pick = lax.broadcasted_iota(jnp.int32, (1, 2), 1)
    combined[...] = jnp.where(
        pick == 0, root * (weighted_sum / weight_sum), root * (jnp.sqrt(weight_sum + 2.0 * pair_sum) / weight_sum)
    )

    for axis, (count, mine, peer) in enumerate(axes):
        for d in range(1, count):
            pltpu.make_async_remote_copy(
                src_ref=gath.at[axis, mine], dst_ref=gath.at[axis, mine],
                send_sem=g_send.at[axis, d], recv_sem=g_recv.at[axis, mine],
                device_id=(peer(lax.rem(mine + d, count)), det), device_id_type=MESH,
            ).wait_send()

    @pl.when(jnp.logical_not(first))
    def _():
        for p in range(2):
            half_copy(p).wait_send()

    flag_copy().wait_send()
    for which in range(3):
        power_copy(which).wait_send()
    for s in range(SEG):
        out_copy(s).wait()
        for q in range(2):
            x_copy(s, q).wait_send()
    sum_copy.wait_send()


def on_device(dims, strain, final_half, intersection_function, notch_mask, quality_flags):
    window, ones, twist, twos = tables()
    any_space = pl.BlockSpec(memory_space=pl.ANY)
    vmem = pl.BlockSpec(memory_space=pltpu.VMEM)
    smem = pl.BlockSpec(memory_space=pltpu.SMEM)
    dma = pltpu.SemaphoreType.DMA
    csd, stats, combined = pl.pallas_call(
        functools.partial(kernel, dims),
        out_shape=(
            jax.ShapeDtypeStruct((SEG, 128, 128), F32),
            jax.ShapeDtypeStruct((3, SEG), F32),
            jax.ShapeDtypeStruct((1, 2), F32),
        ),
        in_specs=[any_space, any_space, any_space, any_space, smem, any_space, any_space, any_space, any_space],
        out_specs=(any_space, vmem, vmem),
        scratch_shapes=[
            pltpu.VMEM((SEG + 1, HALF, COLS), F32),
            pltpu.VMEM((HALF, COLS), F32),
            pltpu.VMEM((2, FULL, 3 * KPAD), BF16),
            pltpu.VMEM((2, 2, HALF, COLS), F32),
            pltpu.VMEM((2, 3 * COLS, 256), BF16),
            pltpu.VMEM((64, 128), F32),
            pltpu.VMEM((64, 128), jnp.int32),
            pltpu.VMEM((2, 3 * KPAD, COLS), BF16),
            pltpu.VMEM((2, FULL, COLS), F32),
            pltpu.VMEM((2, FULL, 3 * COLS), BF16),
            pltpu.VMEM((SEG, 2, 2, FULL, 128), F32),
            pltpu.VMEM((SEG, 2, FULL, 128), F32),
            pltpu.VMEM((SEG, 2, 64, 128), F32),
            pltpu.VMEM((2, 2, 64, 128), F32),
            pltpu.VMEM((2, 64, 128), F32),
            pltpu.VMEM((SEG, 128, 128), F32),
            pltpu.VMEM((16, 128), F32),
            pltpu.VMEM((16, 128), F32),
            pltpu.VMEM((3, 8, 8, 128), F32),
            pltpu.VMEM((8, 128), F32),
            pltpu.VMEM((8, 128), F32),
            pltpu.VMEM((128, 128), F32),
            pltpu.VMEM((SEG, 64, 128), F32),
            dma((20,)),
            dma((2,)),
            dma((2,)),
            dma((SEG, 2)),
            dma((SEG, 2)),
            dma((4,)),
            dma((4,)),
            dma((2,)),
            dma((3, 8)),
            dma((3, 8)),
            dma((SEG + 1,)),
        ],
        compiler_params=pltpu.CompilerParams(
            collective_id=0, has_side_effects=True, vmem_limit_bytes=67_043_328
        ),
    )(
        strain,
        final_half,
        intersection_function.reshape(64, 128),
        notch_mask.reshape(64, 128),
        quality_flags,
        window,
        ones,
        twist,
        twos,
    )
    csd = csd.reshape(SEG, 64, 2, 128).transpose(0, 2, 1, 3).reshape(SEG, 2, 64 * 128)
    return csd, stats, combined.reshape(2)


def solution(mesh):
    count = mesh.shape["tm"]
    dims = (4, 8, 8) if count == 256 else (2, 2, count // 4)
    return jax.shard_map(
        functools.partial(on_device, dims),
        mesh=mesh,
        in_specs=(P("det", "tm", None, None), P("det", None, None), P("det"), P("det"), P("tm")),
        out_specs=(P("tm", None, "det"), P(None, "tm"), P()),
        check_vma=False,
    )
```

profile of v0, /device:TPU:1, one launch (start us, length us, event | category | flops | bytes accessed | tf_op | source)
XLA Modules:
  0.0 54.3 jit_solution(6175316590566214568)
XLA Ops:
  0.6 49.6 %shard_map.112 = (f32[4,128,128]{2,1,0:T(8,128)}, f32[3,4]{1,0:T(4,128)}, f32[1,2]{1,0:T(1,128)}) custom-call(f32[1,4,192,512]{3,2,1,0:T(8,128)} %strain.1, f32[1,192,512]{2,1,0:T(8,128)} %final.1, f32[64,128]{1,0:T(8,128)} %bitcast.9, s32[64,128]{1,0:T(8,128)} %bitcast.10, s32[4]{0:T(128)} %flags.1, f32[192,512]{1,0:T(8,128)} %constant.8.clone.window, ...), custom_call_target="tpu_custom_call" | custom-call | tf_op jit(solution)/shard_map/pallas_call | solution.py:436
  50.3 1.7 %copy.16 = f32[4,2,8192]{2,1,0:T(2,128)} copy(f32[4,2,8192]{2,1,0:T(2,128)} %bitcast.8) | data formatting | bytes 524288
  51.9 1.2 %copy.17 = f32[3,4]{1,0:T(4,128)} copy(f32[3,4]{1,0:T(4,128)} %get-tuple-element.13) | data formatting | bytes 96
  53.2 1.1 %copy.18 = f32[2]{0:T(128)} copy(f32[2]{0:T(128)} %bitcast.11) | data formatting | bytes 16
where the time goes:
time: 54.5 us; the launch traced here: 54.3 us
  Pallas kernels  49.6 us (91%)
  local copies, waits for them, and re-layouts  4 us (7%)
  between operations  0.64 us (1%)
    pallas_call x1, Pallas kernels, on_device(): pl.pallas_call(functools.partial(kernel, dims), out_shape=(jax.ShapeDtype...  49.6 us
    unnamed x3, local copies, waits for them, and re-layouts  4 us

commit v1 on v0

v1 whole, which is shorter than its diff:
```python
import functools

import jax
import jax.numpy as jnp
import numpy as np
from jax import lax
from jax.experimental import pallas as pl
from jax.experimental.pallas import tpu as pltpu
from jax.sharding import PartitionSpec as P

MESH = pl.DeviceIdType.MESH
F32 = jnp.float32
BF16 = jnp.bfloat16

HALF = 192
FULL = 384
COLS = 512
LENGTH = FULL * COLS
KBLK = 256
BIN = 6
GROUPS = FULL // BIN
COARSE = 16384
KPAD = 256
CORR = 27.0 / 154.0
SEG = 4
EVEN, ODD = 112, 96
ROWS = EVEN + ODD


def split_np(table):
    high = table.astype(np.float32).astype(BF16)
    low = (table - high.astype(np.float64)).astype(np.float32).astype(BF16)
    return high, low


@functools.cache
def tables():
    row = np.arange(HALF)
    col = np.arange(COLS)
    window = np.sin(np.pi * (row[:, None] * COLS + col[None, :]) / LENGTH) ** 2

    ones, twists = [], []
    for slabs in (((0, 48, 33), (2, 64, 64)), ((1, 64, 64), (3, 32, 32))):
        bins = np.concatenate([BIN * np.arange(rows) + r for r, rows, _ in slabs])
        keep = np.concatenate([np.arange(rows) < used for _, rows, used in slabs])[:, None]
        angle = 2.0 * np.pi * (bins[:, None] * row[None, :] % FULL) / FULL
        one = np.concatenate([np.cos(angle) * keep, -np.sin(angle) * keep], axis=0)
        ones.append(np.pad(one, ((0, 0), (0, KPAD - HALF))))
        turn = 2.0 * np.pi * (bins[:, None] * col[None, :] % LENGTH) / LENGTH
        twists.append(np.stack([np.cos(turn), np.sin(turn)]))
    one_hi, one_lo = split_np(np.concatenate(ones))

    twos = []
    t = np.arange(32)
    for q in range(4):
        parts = []
        for band in range(2):
            direct, mirrored = 32 * band + t, 127 - 32 * band - t
            k2 = 4 * np.concatenate([direct, mirrored] if q % 2 == 0 else [mirrored, direct]) + q
            angle = 2.0 * np.pi * (np.arange(128)[:, None] * k2[None, :] % COLS) / COLS
            c, s = np.cos(angle), np.sin(angle)
            parts.append(np.concatenate([c, s], axis=0))
            parts.append(np.concatenate([-s, c], axis=0))
        twos.append(np.concatenate(parts, axis=1))
    two_hi, two_lo = split_np(np.stack(twos) * (8.0 / (3.0 * LENGTH) / BIN) ** 0.5)
    return (
        window.astype(np.float32),
        np.stack([one_hi, one_lo]),
        np.concatenate(twists, axis=1).astype(np.float32),
        np.stack([two_hi, two_lo], axis=1),
    )


def kernel(
    dims,
    strain, final, func, mask, flags, window, ones, twist, twos,
    csd, stats, combined,
    h, win, one, twi, two, fnat, mnat, rhs, y, lhs, xb, rb, pw, halo, ob, sums, rsums, gath, fg, re_c,
    load_sem, half_send, half_recv, x_send, x_recv, p_sem, s_sem, g_send, g_recv, o_sem, near_sem, far_sem,
):
    nx, nz, ny = dims
    total = nx * nz * ny
    me = lax.axis_index("tm")
    det = lax.axis_index("det")
    cy = lax.rem(me, ny)
    cz = lax.rem(me // ny, nz)
    cx = me // (ny * nz)
    prev = lax.rem(me + total - 1, total)
    following = lax.rem(me + 1, total)
    first = me == 0
    last = me == total - 1

    def y_peer(k):
        return (cx * nz + cz) * ny + k

    def z_peer(k):
        return (cx * nz + k) * ny + cy

    def x_peer(k):
        return (k * nz + cz) * ny + cy

    axes = ((ny, cy, y_peer), (nz, cz, z_peer), (nx, cx, x_peer))

    barrier = pltpu.get_barrier_semaphore()
    around = [(peer(lax.rem(mine + d, count)), det) for count, mine, peer in axes for d in (1, count - 1)]
    neighbours = [(prev, det), (following, det), (me, 1 - det)] + around
    for peer in neighbours:
        pl.semaphore_signal(barrier, inc=1, device_id=peer, device_id_type=MESH)

    loads = []

    def load(src, dst):
        copy = pltpu.make_async_copy(src, dst, load_sem.at[len(loads)])
        copy.start()
        loads.append(copy)

    load(window, win)
    for s in range(SEG):
        load(strain.at[0, s], h.at[s + 1])
    for part in range(3):
        load(ones.at[part % 2], one.at[:, pl.ds(KPAD * part, KPAD)])
    load(twist, twi)
    for part in range(3):
        load(twos.at[:, (0, 0, 1)[part]], two.at[:, pl.ds(256 * part, 256)])
    load(func, fnat)
    load(mask, mnat)

    gap = jnp.zeros((KPAD - HALF, COLS), BF16)
    for parity in range(2):
        for part in range(3):
            rhs[parity, pl.ds(KPAD * part + HALF, KPAD - HALF), :] = gap
    sums[...] = jnp.zeros((16, 128), F32)

    pl.semaphore_wait(barrier, len(neighbours))

    def half_copy(end, p):
        cols = pl.ds(256 * p, 256)
        source, slot, target = ((0, SEG + 1, prev), (SEG - 1, 0, following))[end]
        return pltpu.make_async_remote_copy(
            src_ref=strain.at[0, source, :, cols],
            dst_ref=h.at[slot, :, cols],
            send_sem=half_send.at[end, p],
            recv_sem=half_recv.at[end, p],
            device_id=(target, det),
            device_id_type=MESH,
        )

    @pl.when(jnp.logical_not(first))
    def _():
        for p in range(2):
            half_copy(0, p).start()

    @pl.when(jnp.logical_not(last))
    def _():
        for p in range(2):
            half_copy(1, p).start()

    def edge_copy(end):
        if end == 0:
            return pltpu.make_async_copy(final.at[0], h.at[SEG + 1], o_sem.at[SEG])
        return pltpu.make_async_copy(strain.at[0, 0], h.at[0], o_sem.at[SEG])

    edges = (last, first)
    for end in range(2):

        @pl.when(edges[end])
        def _(end=end):
            edge_copy(end).start()

    for peer in around:
        pl.semaphore_signal(near_sem, inc=1, device_id=peer, device_id_type=MESH)
    two_away = [
        (peer(lax.rem(mine + d, count)), det) for count, mine, peer in axes if count > 4 for d in (2, count - 2)
    ]

    def report_near():
        pl.semaphore_wait(near_sem, len(around))
        for peer in two_away:
            pl.semaphore_signal(far_sem, inc=1, device_id=peer, device_id_type=MESH)

    def report_far():
        if two_away:
            pl.semaphore_wait(far_sem, len(two_away))

    for copy in loads:
        copy.wait()

    low_lane = lax.broadcasted_iota(jnp.int32, (32, 128), 1) < 64

    blocks = []
    for half in range(2):
        f_half = fnat[pl.ds(half, 32, stride=2), :]
        g_half = f_half * mnat[pl.ds(half, 32, stride=2), :].astype(F32)
        blocks.append(jnp.where(low_lane, f_half, pltpu.roll(g_half, 64, 1)))
        blocks.append(jnp.where(low_lane, pltpu.roll(f_half, 64, 1), g_half))
    fg[...] = jnp.concatenate(blocks, axis=0).T

    def split(value):
        high = value.astype(BF16)
        return high, (value - high.astype(F32)).astype(BF16)

    def transform(s, end=None):
        for p in range(2):
            cols = pl.ds(256 * p, 256)
            if end is not None:

                @pl.when(jnp.logical_not(edges[end]))
                def _():
                    half_copy(end, p).wait_recv()

                if p == 0:

                    @pl.when(edges[end])
                    def _():
                        edge_copy(end).wait()

            def windowed(i, carry):
                rows = pl.ds(pl.multiple_of(16 * i, 16), 16)
                upper = h[s + 1, rows, cols]
                lower = h[s + 2, rows, cols]
                w = win[rows, cols]
                for parity, value in ((0, lower + w * (upper - lower)), (1, w * (upper + lower) - lower)):
                    high, low = split(value)
                    rhs[parity, rows, cols] = high
                    rhs[parity, pl.ds(pl.multiple_of(KPAD + 16 * i, 16), 16), cols] = high
                    rhs[parity, pl.ds(pl.multiple_of(2 * KPAD + 16 * i, 16), 16), cols] = low
                return carry

            lax.fori_loop(0, HALF // 16, windowed, 0)
            y[: 2 * EVEN, cols] = jnp.dot(one[: 2 * EVEN], rhs[0, :, cols], preferred_element_type=F32)
            y[2 * EVEN :, cols] = jnp.dot(one[2 * EVEN :], rhs[1, :, cols], preferred_element_type=F32)

        def turned(real_at, imag_at, i):
            rows = pl.ds(pl.multiple_of(16 * i, 16), 16)
            real = y[pl.ds(pl.multiple_of(16 * i + real_at, 16), 16), :]
            imag = y[pl.ds(pl.multiple_of(16 * i + imag_at, 16), 16), :]
            c = twi[0, rows, :]
            n = twi[1, rows, :]
            zr = real * c + imag * n
            zi = imag * c - real * n
            r0, r1, r2, r3 = (zr[:, 128 * p : 128 * p + 128] for p in range(4))
            i0, i1, i2, i3 = (zi[:, 128 * p : 128 * p + 128] for p in range(4))
            ar, br, cr, dr = r0 + r2, r0 - r2, r1 + r3, r1 - r3
            ai, bi, ci, di = i0 + i2, i0 - i2, i1 + i3, i1 - i3
            quarters = ((ar + cr, ai + ci), (br + di, bi - dr), (ar - cr, ai - ci), (br - di, bi + dr))
            for q, pair in enumerate(quarters):
                for at, z in zip((0, 128), pair):
                    high, low = split(z)
                    lhs[q, rows, pl.ds(at, 128)] = high
                    lhs[q, rows, pl.ds(256 + at, 128)] = low
                    lhs[q, rows, pl.ds(512 + at, 128)] = high

        def turned_even(i, carry):
            turned(0, EVEN, i)
            return carry

        def turned_odd(i, carry):
            turned(EVEN, ROWS, i)
            return carry

        lax.fori_loop(0, EVEN // 16, turned_even, 0)
        lax.fori_loop(EVEN // 16, ROWS // 16, turned_odd, 0)
        for pair in range(2):
            for q in (2 * pair, 2 * pair + 1):
                out = jnp.dot(lhs[q], two[q], preferred_element_type=F32)
                xb[s + 1, 0, q] = out[:, :128]
                xb[s + 1, 1, q] = out[:, 128:]
            x_copy(s, pair).start()

    def x_copy(s, pair):
        return pltpu.make_async_remote_copy(
            src_ref=xb.at[s + 1, 1 - det, pl.ds(2 * pair, 2)], dst_ref=rb.at[s + 1, pl.ds(2 * pair, 2)],
            send_sem=x_send.at[s + 1, pair], recv_sem=x_recv.at[s + 1, pair],
            device_id=(me, 1 - det), device_id_type=MESH,
        )

    sign = 1.0 - 2.0 * det.astype(F32)
    group = lax.broadcasted_iota(jnp.int32, (64, 128), 1) // 32
    lane_sign = jnp.where(group < 2, sign, -sign)
    sublane = lax.broadcasted_iota(jnp.int32, (8, 128), 0)
    inner = lax.broadcasted_iota(jnp.int32, (48, 128), 0) < 31

    def reverse_rows(x):
        out = []
        for i in reversed(range(8)):
            v = pltpu.roll(x[8 * i : 8 * i + 8], 4, 0)
            v = jnp.where((sublane & 2) == 0, pltpu.roll(v, 6, 0), pltpu.roll(v, 2, 0))
            out.append(jnp.where((sublane & 1) == 0, pltpu.roll(v, 7, 0), pltpu.roll(v, 1, 0)))
        return jnp.concatenate(out, axis=0)

    def coarse(product, fold):
        direct = mirrored = direct_0 = mirrored_0 = None
        for q in range(4):
            body = product(q, 48, 64) + product(q, 112, 64)
            body = fold(jnp.concatenate([body[:32] + product(q, 176, 32), body[32:]], axis=0))
            zero = fold(product(q, 0, 48))
            if q == 0:
                direct = mirrored = body
                direct_0 = mirrored_0 = zero
            else:
                direct = jnp.where(group == q, body, direct)
                mirrored = jnp.where(group == 3 - q, body, mirrored)
                direct_0 = jnp.where(group[:48] == q, zero, direct_0)
                mirrored_0 = jnp.where(group[:48] == 3 - q, zero, mirrored_0)
        mirrored_0 = jnp.where(inner, pltpu.roll(mirrored_0, 47, 0), 0.0)
        direct = jnp.concatenate([direct[:48] + direct_0, direct[48:]], axis=0)
        mirrored = jnp.concatenate([mirrored[:48] + mirrored_0, mirrored[48:]], axis=0)
        return direct, reverse_rows(mirrored)

    def plus(x):
        return x + pltpu.roll(x, 64, 1)

    def minus(x):
        return x - pltpu.roll(x, 64, 1)

    def crossed(s):
        def mine(q, at, count):
            return xb[s + 1, det, q, pl.ds(at, count), :]

        def theirs(q, at, count):
            return rb[s + 1, q, pl.ds(at, count), :]

        direct, mirrored = coarse(lambda *where: mine(*where) * mine(*where), plus)
        pw[s + 1, 0] = direct + mirrored
        for pair in range(2):
            x_copy(s, pair).wait_recv()
        direct, mirrored = coarse(lambda *where: theirs(*where) * theirs(*where), plus)
        pw[s + 1, 1] = direct + mirrored
        if s < 0:
            return
        direct, mirrored = coarse(lambda *where: mine(*where) * theirs(*where), plus)
        real = direct + mirrored
        re_c[s] = real
        direct, mirrored = coarse(lambda *where: mine(*where) * pltpu.roll(theirs(*where), 64, 1), minus)
        imag = (direct - mirrored) * lane_sign
        turned = jnp.concatenate([real, imag], axis=0).T
        for half in range(2):
            first_part = turned[64 * half : 64 * half + 32]
            second_part = turned[64 * half + 32 : 64 * half + 64]
            ob[s, pl.ds(2 * half, 32, stride=4), :] = jnp.where(low_lane, first_part, pltpu.roll(second_part, 64, 1))
            ob[s, pl.ds(2 * half + 1, 32, stride=4), :] = jnp.where(
                low_lane, pltpu.roll(first_part, 64, 1), second_part
            )
        out_copy(s).start()

    def out_copy(s):
        return pltpu.make_async_copy(ob.at[s], csd.at[s], o_sem.at[s])

    power_copy = pltpu.make_async_remote_copy(
        src_ref=pw.at[1], dst_ref=halo, send_sem=p_sem.at[0], recv_sem=p_sem.at[1],
        device_id=(prev, det), device_id_type=MESH,
    )

    transform(0)
    transform(1)
    report_near()
    crossed(0)
    transform(2)
    report_far()
    crossed(1)
    crossed(2)
    transform(SEG - 1, 0)
    power_copy.start()
    transform(-1, 1)
    crossed(SEG - 1)

    f_t = fg[pl.ds(0, 64), :]
    g_t = fg[pl.ds(64, 64), :]

    def accumulate(s, left, right, weight_left, weight_right):
        mean_a = left(0) * weight_left + right(0) * weight_right
        mean_b = left(1) * weight_left + right(1) * weight_right
        filt = g_t / (mean_a * mean_b)
        sums[pl.ds(s, 1), :] = jnp.sum(filt * re_c[s], axis=0, keepdims=True)
        sums[pl.ds(8 + s, 1), :] = jnp.sum(filt * f_t, axis=0, keepdims=True)

    def own(s):
        return lambda a: pw[s + 1, a]

    for s in (1, 2):
        accumulate(s, own(s - 1), own(s + 1), 0.5, 0.5)
    crossed(-1)
    starts = jnp.where(first, 1.0, 0.5).astype(F32)
    accumulate(0, own(-1), own(1), 1.0 - starts, starts)
    power_copy.wait_recv()
    ends = jnp.where(last, 1.0, 0.5).astype(F32)
    accumulate(SEG - 1, own(SEG - 2), lambda a: halo[a], ends, 1.0 - ends)

    sum_copy = pltpu.make_async_remote_copy(
        src_ref=sums, dst_ref=rsums, send_sem=s_sem.at[0], recv_sem=s_sem.at[1],
        device_id=(me, 1 - det), device_id_type=MESH,
    )
    sum_copy.start()
    lane = lax.broadcasted_iota(jnp.int32, (8, 128), 1)
    row = lax.broadcasted_iota(jnp.int32, (8, 128), 0)
    quality = jnp.zeros((8, 128), F32)
    for s in range(SEG):
        quality = jnp.where(lane == s, flags[s].astype(F32), quality)
    sum_copy.wait_recv()
    whole = jnp.sum(sums[...] + rsums[...], axis=1, keepdims=True)

    def to_lanes(column):
        spread_out = jnp.where(lane == row, jnp.broadcast_to(column, (8, 128)), 0.0)
        return jnp.broadcast_to(jnp.sum(spread_out, axis=0, keepdims=True), (8, 128))

    numerator = to_lanes(whole[:8])
    denominator = to_lanes(whole[8:])
    spread = jnp.sqrt(float(COARSE) / denominator)
    estimate = float(np.sqrt(12.0 * COARSE)) * numerator / denominator
    weight = quality / (spread * spread)
    per_spread = quality / spread
    up = quality * spread
    inside = lane < SEG - 1
    covariance = CORR * up * pltpu.roll(up, 127, 1)
    pair_term = jnp.where(inside, CORR * per_spread * pltpu.roll(per_spread, 127, 1), 0.0)

    rows = [weight, weight * estimate, pair_term, pltpu.roll(per_spread, SEG - 1, 1), per_spread, pltpu.roll(up, SEG - 1, 1)]
    terms = jnp.zeros((8, 128), F32)
    for i, value in enumerate(rows):
        terms = jnp.where(row == i, value, terms)
    terms = jnp.where((lane < SEG) & ((row < 3) | (lane == SEG - 1)), terms, 0.0)
    next_first = jnp.zeros((8, 128), F32)
    open_end = None

    for axis, (count, mine, peer) in enumerate(axes):
        gath[axis, mine] = terms

        def gather_copy(d, axis=axis, count=count, mine=mine, peer=peer):
            return pltpu.make_async_remote_copy(
                src_ref=gath.at[axis, mine], dst_ref=gath.at[axis, mine],
                send_sem=g_send.at[axis, d], recv_sem=g_recv.at[axis, mine],
                device_id=(peer(lax.rem(mine + d, count)), det), device_id_type=MESH,
            )

        for d in range(1, count):
            gather_copy(d).start()
        for d in range(1, count):
            source = lax.rem(mine + d, count)
            pltpu.make_async_remote_copy(
                src_ref=gath.at[axis, source], dst_ref=gath.at[axis, source],
                send_sem=g_send.at[axis, d], recv_sem=g_recv.at[axis, source],
                device_id=(peer(source), det), device_id_type=MESH,
            ).wait_recv()
        groups = [gath[axis, k] for k in range(count)]
        total_terms, joints = groups[0], jnp.zeros((8, 128), F32)
        for before, after in zip(groups[:-1], groups[1:]):
            total_terms = total_terms + after
            joints = joints + before * pltpu.roll(after, 1, 0)
        total_terms = total_terms + jnp.where(row == 2, CORR * pltpu.roll(joints, 6, 0), 0.0)
        terms = jnp.where(row < 3, total_terms, jnp.where(row == 4, groups[-1], groups[0]))
        here = mine < count - 1
        if open_end is not None:
            here = jnp.logical_and(open_end, here)
        next_first = jnp.where(here, gath[axis, jnp.minimum(mine + 1, count - 1)], next_first)
        at_end = mine == count - 1
        open_end = at_end if open_end is None else jnp.logical_and(open_end, at_end)

    covariance = jnp.where(inside, covariance, CORR * up * pltpu.roll(next_first, 5, 0))
    rows3 = jnp.where(row == 0, estimate, jnp.where(row == 1, spread, covariance))
    stats[...] = rows3[:3, :SEG]

    sweep = jnp.sum(terms, axis=1, keepdims=True)
    weight_sum, weighted_sum, pair_sum = sweep[0:1], sweep[1:2], sweep[2:3]
    root = float(np.sqrt(SEG * total))
    pick = lax.broadcasted_iota(jnp.int32, (1, 2), 1)
    combined[...] = jnp.where(
        pick == 0, root * (weighted_sum / weight_sum), root * (jnp.sqrt(weight_sum + 2.0 * pair_sum) / weight_sum)
    )

    for axis, (count, mine, peer) in enumerate(axes):
        for d in range(1, count):
            pltpu.make_async_remote_copy(
                src_ref=gath.at[axis, mine], dst_ref=gath.at[axis, mine],
                send_sem=g_send.at[axis, d], recv_sem=g_recv.at[axis, mine],
                device_id=(peer(lax.rem(mine + d, count)), det), device_id_type=MESH,
            ).wait_send()

    for end in range(2):

        @pl.when(jnp.logical_not(edges[1 - end]))
        def _(end=end):
            for p in range(2):
                half_copy(end, p).wait_send()

    power_copy.wait_send()
    for s in range(SEG):
        out_copy(s).wait()
    for s in range(-1, SEG):
        for pair in range(2):
            x_copy(s, pair).wait_send()
    sum_copy.wait_send()


def writer(csd_in, stats_in, combined_in, csd, stats, combined, csd_v, stats_v, combined_v, sems):
    held = (csd_v, stats_v, combined_v)
    for way, pairs in enumerate((zip((csd_in, stats_in, combined_in), held), zip(held, (csd, stats, combined)))):
        copies = [pltpu.make_async_copy(src, dst, sems.at[way, i]) for i, (src, dst) in enumerate(pairs)]
        for copy in copies:
            copy.start()
        for copy in copies:
            copy.wait()


def on_device(dims, strain, final_half, intersection_function, notch_mask, quality_flags):
    window, ones, twist, twos = tables()
    any_space = pl.BlockSpec(memory_space=pl.ANY)
    hbm = pl.BlockSpec(memory_space=pltpu.HBM)
    vmem = pl.BlockSpec(memory_space=pltpu.VMEM)
    smem = pl.BlockSpec(memory_space=pltpu.SMEM)
    dma = pltpu.SemaphoreType.DMA
    csd, stats, combined = pl.pallas_call(
        functools.partial(kernel, dims),
        out_shape=(
            jax.ShapeDtypeStruct((SEG, 128, 128), F32),
            jax.ShapeDtypeStruct((3, SEG), F32),
            jax.ShapeDtypeStruct((1, 2), F32),
        ),
        in_specs=[hbm, hbm, hbm, hbm, smem, hbm, hbm, hbm, hbm],
        out_specs=(any_space, vmem, vmem),
        scratch_shapes=[
            pltpu.VMEM((SEG + 2, HALF, COLS), F32),
            pltpu.VMEM((HALF, COLS), F32),
            pltpu.VMEM((2 * ROWS, 3 * KPAD), BF16),
            pltpu.VMEM((2, ROWS, COLS), F32),
            pltpu.VMEM((4, 3 * 256, 256), BF16),
            pltpu.VMEM((64, 128), F32),
            pltpu.VMEM((64, 128), jnp.int32),
            pltpu.VMEM((2, 3 * KPAD, COLS), BF16),
            pltpu.VMEM((2 * ROWS, COLS), F32),
            pltpu.VMEM((4, ROWS, 3 * 256), BF16),
            pltpu.VMEM((SEG + 1, 2, 4, ROWS, 128), F32),
            pltpu.VMEM((SEG + 1, 4, ROWS, 128), F32),
            pltpu.VMEM((SEG + 1, 2, 64, 128), F32),
            pltpu.VMEM((2, 64, 128), F32),
            pltpu.VMEM((SEG, 128, 128), F32),
            pltpu.VMEM((16, 128), F32),
            pltpu.VMEM((16, 128), F32),
            pltpu.VMEM((3, 8, 8, 128), F32),
            pltpu.VMEM((128, 128), F32),
            pltpu.VMEM((SEG, 64, 128), F32),
            dma((20,)),
            dma((2, 2)),
            dma((2, 2)),
            dma((SEG + 1, 2)),
            dma((SEG + 1, 2)),
            dma((2,)),
            dma((2,)),
            dma((3, 8)),
            dma((3, 8)),
            dma((SEG + 1,)),
            pltpu.SemaphoreType.REGULAR,
            pltpu.SemaphoreType.REGULAR,
        ],
        compiler_params=pltpu.CompilerParams(
            collective_id=0, has_side_effects=True, vmem_limit_bytes=67_043_328
        ),
    )(
        strain,
        final_half,
        intersection_function.reshape(64, 128),
        notch_mask.reshape(64, 128),
        quality_flags,
        window,
        ones,
        twist,
        twos,
    )
    csd, stats, combined = pl.pallas_call(
        writer,
        out_shape=(
            jax.ShapeDtypeStruct((SEG, 128, 128), F32),
            jax.ShapeDtypeStruct((3, SEG), F32),
            jax.ShapeDtypeStruct((1, 2), F32),
        ),
        in_specs=[any_space] * 3,
        out_specs=[any_space] * 3,
        scratch_shapes=[
            pltpu.VMEM((SEG, 128, 128), F32),
            pltpu.VMEM((3, SEG), F32),
            pltpu.VMEM((1, 2), F32),
            dma((2, 3)),
        ],
    )(csd, stats, combined)
    csd = csd.reshape(SEG, 64, 2, 128).transpose(0, 2, 1, 3).reshape(SEG, 2, 64 * 128)
    return csd, stats, combined.reshape(2)


def solution(mesh):
    count = mesh.shape["tm"]
    dims = (4, 8, 8) if count == 256 else (2, 2, count // 4)
    return jax.shard_map(
        functools.partial(on_device, dims),
        mesh=mesh,
        in_specs=(P("det", "tm", None, None), P("det", None, None), P("det"), P("det"), P("tm")),
        out_specs=(P("tm", None, "det"), P(None, "tm"), P()),
        check_vma=False,
    )
```

time: 54.5 us -> 47.5 us (0.87)
  the two profiles are of different devices: /device:TPU:1 before, /device:TPU:8 now
where the time goes in v1:
time: 47.5 us; the launch traced here: 47.4 us
  Pallas kernels  46.7 us (98%)
  between operations  0.64 us (1%)
    pallas_call x1, Pallas kernels, on_device(): pl.pallas_call(functools.partial(kernel, dims), out_shape=(jax.ShapeDtype...  45 us
    pallas_call x1, Pallas kernels, on_device(): pl.pallas_call(writer, out_shape=(jax.ShapeDtypeStruct((SEG, 128, 128), F...  1.71 us

profile of v1, /device:TPU:8, one launch (start us, length us, event | category | flops | bytes accessed | tf_op | source)
XLA Modules:
  0.0 47.4 jit_solution(1438388266336944564)
XLA Ops:
  0.6 45.0 %shard_map.112 = (f32[4,128,128]{2,1,0:T(8,128)}, f32[3,4]{1,0:T(4,128)}, f32[1,2]{1,0:T(1,128)}) custom-call(f32[1,4,192,512]{3,2,1,0:T(8,128)} %strain.1, f32[1,192,512]{2,1,0:T(8,128)} %final.1, f32[64,128]{1,0:T(8,128)} %bitcast.8, s32[64,128]{1,0:T(8,128)} %bitcast.9, s32[4]{0:T(128)} %flags.1, f32[192,512]{1,0:T(8,128)} %constant.8.clone.window, ...), custom_call_target="tpu_custom_call" | custom-call | tf_op jit(solution)/shard_map/pallas_call | solution.py:511
  45.7 1.7 %shard_map.113 = (f32[4,128,128]{2,1,0:T(8,128)}, f32[3,4]{1,0:T(4,128)}, f32[1,2]{1,0:T(1,128)}) custom-call(f32[4,128,128]{2,1,0:T(8,128)} %get-tuple-element.9.csd_in, f32[3,4]{1,0:T(4,128)} %get-tuple-element.10.stats_in, f32[1,2]{1,0:T(1,128)} %get-tuple-element.11.combined_in), custom_call_target="tpu_custom_call" | custom-call | tf_op jit(solution)/shard_map/pallas_call | solution.py:568

commit v2 on v1

--- a/solution.py
+++ b/solution.py
@@ -73,9 +73,9 @@
 
 def kernel(
     dims,
-    strain, final, func, mask, flags, window, ones, twist, twos,
+    strain, final, func, mask, flags_in, window, ones, twist, twos,
     csd, stats, combined,
-    h, win, one, twi, two, fnat, mnat, rhs, y, lhs, xb, rb, pw, halo, ob, sums, rsums, gath, fg, re_c,
+    h, win, one, twi, two, fnat, mnat, rhs, y, lhs, xb, rb, pw, halo, ob, sums, rsums, gath, fg, re_c, flags,
     load_sem, half_send, half_recv, x_send, x_recv, p_sem, s_sem, g_send, g_recv, o_sem, near_sem, far_sem,
 ):
     nx, nz, ny = dims
@@ -113,17 +113,15 @@
         copy = pltpu.make_async_copy(src, dst, load_sem.at[len(loads)])
         copy.start()
         loads.append(copy)
-
-    load(window, win)
-    for s in range(SEG):
-        load(strain.at[0, s], h.at[s + 1])
-    for part in range(3):
-        load(ones.at[part % 2], one.at[:, pl.ds(KPAD * part, KPAD)])
-    load(twist, twi)
-    for part in range(3):
-        load(twos.at[:, (0, 0, 1)[part]], two.at[:, pl.ds(256 * part, 256)])
-    load(func, fnat)
-    load(mask, mnat)
+        return copy
+
+    outgoing = [load(strain.at[0, s], h.at[s + 1]) for s in (0, SEG - 1)]
+    early = [load(window, win), load(strain.at[0, 1], h.at[2])]
+    early += [load(ones.at[part % 2], one.at[:, pl.ds(KPAD * part, KPAD)]) for part in range(3)]
+    twist_load = load(twist, twi)
+    two_loads = [load(twos.at[:, (0, 0, 1)[part]], two.at[:, pl.ds(256 * part, 256)]) for part in range(3)]
+    late = [load(strain.at[0, s], h.at[s + 1]) for s in range(2, SEG - 1)]
+    late += [load(func, fnat), load(mask, mnat), load(flags_in, flags)]
 
     gap = jnp.zeros((KPAD - HALF, COLS), BF16)
     for parity in range(2):
@@ -137,7 +135,7 @@
         cols = pl.ds(256 * p, 256)
         source, slot, target = ((0, SEG + 1, prev), (SEG - 1, 0, following))[end]
         return pltpu.make_async_remote_copy(
-            src_ref=strain.at[0, source, :, cols],
+            src_ref=h.at[source + 1, :, cols],
             dst_ref=h.at[slot, :, cols],
             send_sem=half_send.at[end, p],
             recv_sem=half_recv.at[end, p],
@@ -145,6 +143,9 @@
             device_id_type=MESH,
         )
 
+    for copy in outgoing:
+        copy.wait()
+
     @pl.when(jnp.logical_not(first))
     def _():
         for p in range(2):
@@ -182,58 +183,46 @@
         if two_away:
             pl.semaphore_wait(far_sem, len(two_away))
 
-    for copy in loads:
-        copy.wait()
-
-    low_lane = lax.broadcasted_iota(jnp.int32, (32, 128), 1) < 64
-
-    blocks = []
-    for half in range(2):
-        f_half = fnat[pl.ds(half, 32, stride=2), :]
-        g_half = f_half * mnat[pl.ds(half, 32, stride=2), :].astype(F32)
-        blocks.append(jnp.where(low_lane, f_half, pltpu.roll(g_half, 64, 1)))
-        blocks.append(jnp.where(low_lane, pltpu.roll(f_half, 64, 1), g_half))
-    fg[...] = jnp.concatenate(blocks, axis=0).T
-
     def split(value):
         high = value.astype(BF16)
         return high, (value - high.astype(F32)).astype(BF16)
 
-    def transform(s, end=None):
-        for p in range(2):
-            cols = pl.ds(256 * p, 256)
-            if end is not None:
-
-                @pl.when(jnp.logical_not(edges[end]))
+    def first_stage(s, p, slot=0, end=None):
+        cols = pl.ds(256 * p, 256)
+        if end is not None:
+
+            @pl.when(jnp.logical_not(edges[end]))
+            def _():
+                half_copy(end, p).wait_recv()
+
+            if p == 0:
+
+                @pl.when(edges[end])
                 def _():
-                    half_copy(end, p).wait_recv()
-
-                if p == 0:
-
-                    @pl.when(edges[end])
-                    def _():
-                        edge_copy(end).wait()
-
-            def windowed(i, carry):
-                rows = pl.ds(pl.multiple_of(16 * i, 16), 16)
-                upper = h[s + 1, rows, cols]
-                lower = h[s + 2, rows, cols]
-                w = win[rows, cols]
-                for parity, value in ((0, lower + w * (upper - lower)), (1, w * (upper + lower) - lower)):
-                    high, low = split(value)
-                    rhs[parity, rows, cols] = high
-                    rhs[parity, pl.ds(pl.multiple_of(KPAD + 16 * i, 16), 16), cols] = high
-                    rhs[parity, pl.ds(pl.multiple_of(2 * KPAD + 16 * i, 16), 16), cols] = low
-                return carry
-
-            lax.fori_loop(0, HALF // 16, windowed, 0)
-            y[: 2 * EVEN, cols] = jnp.dot(one[: 2 * EVEN], rhs[0, :, cols], preferred_element_type=F32)
-            y[2 * EVEN :, cols] = jnp.dot(one[2 * EVEN :], rhs[1, :, cols], preferred_element_type=F32)
-
+                    edge_copy(end).wait()
+
+        def windowed(i, carry):
+            rows = pl.ds(16 * i, 16)
+            upper = h[s + 1, rows, cols]
+            lower = h[s + 2, rows, cols]
+            w = win[rows, cols]
+            for parity, value in ((0, lower + w * (upper - lower)), (1, w * (upper + lower) - lower)):
+                high, low = split(value)
+                rhs[parity, rows, cols] = high
+                rhs[parity, pl.ds(KPAD + 16 * i, 16), cols] = high
+                rhs[parity, pl.ds(2 * KPAD + 16 * i, 16), cols] = low
+            return carry
+
+        for i in range(HALF // 16):
+            windowed(i, 0)
+        y[slot, : 2 * EVEN, cols] = jnp.dot(one[: 2 * EVEN], rhs[0, :, cols], preferred_element_type=F32)
+        y[slot, 2 * EVEN :, cols] = jnp.dot(one[2 * EVEN :], rhs[1, :, cols], preferred_element_type=F32)
+
+    def second_stage(s, slot=0):
         def turned(real_at, imag_at, i):
-            rows = pl.ds(pl.multiple_of(16 * i, 16), 16)
-            real = y[pl.ds(pl.multiple_of(16 * i + real_at, 16), 16), :]
-            imag = y[pl.ds(pl.multiple_of(16 * i + imag_at, 16), 16), :]
+            rows = pl.ds(16 * i, 16)
+            real = y[slot, pl.ds(16 * i + real_at, 16), :]
+            imag = y[slot, pl.ds(16 * i + imag_at, 16), :]
             c = twi[0, rows, :]
             n = twi[1, rows, :]
             zr = real * c + imag * n
@@ -258,8 +247,8 @@
             turned(EVEN, ROWS, i)
             return carry
 
-        lax.fori_loop(0, EVEN // 16, turned_even, 0)
-        lax.fori_loop(EVEN // 16, ROWS // 16, turned_odd, 0)
+        for i in range(ROWS // 16):
+            (turned_even if i < EVEN // 16 else turned_odd)(i, 0)
         for pair in range(2):
             for q in (2 * pair, 2 * pair + 1):
                 out = jnp.dot(lhs[q], two[q], preferred_element_type=F32)
@@ -274,6 +263,7 @@
             device_id=(me, 1 - det), device_id_type=MESH,
         )
 
+    low_lane = lax.broadcasted_iota(jnp.int32, (32, 128), 1) < 64
     sign = 1.0 - 2.0 * det.astype(F32)
     group = lax.broadcasted_iota(jnp.int32, (64, 128), 1) // 32
     lane_sign = jnp.where(group < 2, sign, -sign)
@@ -313,13 +303,17 @@
     def minus(x):
         return x - pltpu.roll(x, 64, 1)
 
-    def crossed(s):
+    def spectra(s):
         def mine(q, at, count):
             return xb[s + 1, det, q, pl.ds(at, count), :]
 
         def theirs(q, at, count):
             return rb[s + 1, q, pl.ds(at, count), :]
 
+        return mine, theirs
+
+    def crossed(s):
+        mine, theirs = spectra(s)
         direct, mirrored = coarse(lambda *where: mine(*where) * mine(*where), plus)
         pw[s + 1, 0] = direct + mirrored
         for pair in range(2):
@@ -329,11 +323,13 @@
         if s < 0:
             return
         direct, mirrored = coarse(lambda *where: mine(*where) * theirs(*where), plus)
-        real = direct + mirrored
-        re_c[s] = real
+        re_c[s] = direct + mirrored
+
+    def finished(s):
+        mine, theirs = spectra(s)
         direct, mirrored = coarse(lambda *where: mine(*where) * pltpu.roll(theirs(*where), 64, 1), minus)
         imag = (direct - mirrored) * lane_sign
-        turned = jnp.concatenate([real, imag], axis=0).T
+        turned = jnp.concatenate([re_c[s], imag], axis=0).T
         for half in range(2):
             first_part = turned[64 * half : 64 * half + 32]
             second_part = turned[64 * half + 32 : 64 * half + 64]
@@ -351,18 +347,44 @@
         device_id=(prev, det), device_id_type=MESH,
     )
 
-    transform(0)
-    transform(1)
+    for copy in early:
+        copy.wait()
+    first_stage(0, 0)
+    first_stage(0, 1)
+    twist_load.wait()
+    for copy in two_loads:
+        copy.wait()
+    second_stage(0)
+    for copy in late:
+        copy.wait()
+    first_stage(1, 0)
+    first_stage(1, 1)
+    second_stage(1)
     report_near()
     crossed(0)
-    transform(2)
+    power_copy.start()
+    first_stage(2, 0)
+    first_stage(2, 1)
+    second_stage(2)
     report_far()
+    first_stage(-1, 0, 2, 1)
+    first_stage(SEG - 1, 0, 1, 0)
     crossed(1)
     crossed(2)
-    transform(SEG - 1, 0)
-    power_copy.start()
-    transform(-1, 1)
-    crossed(SEG - 1)
+
+
+    blocks = []
+    for half in range(2):
+        f_half = fnat[pl.ds(half, 32, stride=2), :]
+        g_half = f_half * mnat[pl.ds(half, 32, stride=2), :].astype(F32)
+        blocks.append(jnp.where(low_lane, f_half, pltpu.roll(g_half, 64, 1)))
+        blocks.append(jnp.where(low_lane, pltpu.roll(f_half, 64, 1), g_half))
+    fg[...] = jnp.concatenate(blocks, axis=0).T
+    first_stage(-1, 1, 2, 1)
+    second_stage(-1, 2)
+    first_stage(SEG - 1, 1, 1, 0)
+    second_stage(SEG - 1, 1)
+    crossed(-1)
 
     f_t = fg[pl.ds(0, 64), :]
     g_t = fg[pl.ds(64, 64), :]
@@ -377,14 +399,14 @@
     def own(s):
         return lambda a: pw[s + 1, a]
 
-    for s in (1, 2):
-        accumulate(s, own(s - 1), own(s + 1), 0.5, 0.5)
-    crossed(-1)
     starts = jnp.where(first, 1.0, 0.5).astype(F32)
+    ends = jnp.where(last, 1.0, 0.5).astype(F32)
+    accumulate(1, own(0), own(2), 0.5, 0.5)
     accumulate(0, own(-1), own(1), 1.0 - starts, starts)
     power_copy.wait_recv()
-    ends = jnp.where(last, 1.0, 0.5).astype(F32)
+    crossed(SEG - 1)
     accumulate(SEG - 1, own(SEG - 2), lambda a: halo[a], ends, 1.0 - ends)
+    accumulate(SEG - 2, own(SEG - 3), own(SEG - 1), 0.5, 0.5)
 
     sum_copy = pltpu.make_async_remote_copy(
         src_ref=sums, dst_ref=rsums, send_sem=s_sem.at[0], recv_sem=s_sem.at[1],
@@ -434,6 +456,8 @@
 
         for d in range(1, count):
             gather_copy(d).start()
+        for s in ((0, 1), (2, 3), ())[axis]:
+            finished(s)
         for d in range(1, count):
             source = lax.rem(mine + d, count)
             pltpu.make_async_remote_copy(
@@ -506,7 +530,6 @@
     any_space = pl.BlockSpec(memory_space=pl.ANY)
     hbm = pl.BlockSpec(memory_space=pltpu.HBM)
     vmem = pl.BlockSpec(memory_space=pltpu.VMEM)
-    smem = pl.BlockSpec(memory_space=pltpu.SMEM)
     dma = pltpu.SemaphoreType.DMA
     csd, stats, combined = pl.pallas_call(
         functools.partial(kernel, dims),
@@ -515,7 +538,7 @@
             jax.ShapeDtypeStruct((3, SEG), F32),
             jax.ShapeDtypeStruct((1, 2), F32),
         ),
-        in_specs=[hbm, hbm, hbm, hbm, smem, hbm, hbm, hbm, hbm],
+        in_specs=[hbm] * 9,
         out_specs=(any_space, vmem, vmem),
         scratch_shapes=[
             pltpu.VMEM((SEG + 2, HALF, COLS), F32),
@@ -526,7 +549,7 @@
             pltpu.VMEM((64, 128), F32),
             pltpu.VMEM((64, 128), jnp.int32),
             pltpu.VMEM((2, 3 * KPAD, COLS), BF16),
-            pltpu.VMEM((2 * ROWS, COLS), F32),
+            pltpu.VMEM((3, 2 * ROWS, COLS), F32),
             pltpu.VMEM((4, ROWS, 3 * 256), BF16),
             pltpu.VMEM((SEG + 1, 2, 4, ROWS, 128), F32),
             pltpu.VMEM((SEG + 1, 4, ROWS, 128), F32),
@@ -538,6 +561,7 @@
             pltpu.VMEM((3, 8, 8, 128), F32),
             pltpu.VMEM((128, 128), F32),
             pltpu.VMEM((SEG, 64, 128), F32),
+            pltpu.SMEM((SEG,), jnp.int32),
             dma((20,)),
             dma((2, 2)),
             dma((2, 2)),

time: 47.5 us -> 44.8 us (0.943)
  Pallas kernels: 46.7 us -> 44.1 us
    pallas_call x1, Pallas kernels: 45 us -> 42.3 us  [on_device(): pl.pallas_call(functools.partial(kernel, dims), out_shape=(jax.ShapeDtype...]
where the time goes in v2:
time: 44.8 us; the launch traced here: 44.7 us
  Pallas kernels  44.1 us (98%)
  between operations  0.64 us (1%)
    pallas_call x1, Pallas kernels, on_device(): pl.pallas_call(functools.partial(kernel, dims), out_shape=(jax.ShapeDtype...  42.3 us
    pallas_call x1, Pallas kernels, on_device(): pl.pallas_call(writer, out_shape=(jax.ShapeDtypeStruct((SEG, 128, 128), F...  1.71 us

profile of v2, /device:TPU:8, one launch (start us, length us, event | category | flops | bytes accessed | tf_op | source)
XLA Modules:
  0.0 44.7 jit_solution(10148745352650595685)
XLA Ops:
  0.6 42.3 %shard_map.112 = (f32[4,128,128]{2,1,0:T(8,128)}, f32[3,4]{1,0:T(4,128)}, f32[1,2]{1,0:T(1,128)}) custom-call(f32[1,4,192,512]{3,2,1,0:T(8,128)} %strain.1, f32[1,192,512]{2,1,0:T(8,128)} %final.1, f32[64,128]{1,0:T(8,128)} %bitcast.8, s32[64,128]{1,0:T(8,128)} %bitcast.9, s32[4]{0:T(128)} %flags_in.1, f32[192,512]{1,0:T(8,128)} %constant.8.clone.window, ...), custom_call_target="tpu_custom_call" | custom-call | tf_op jit(solution)/shard_map/pallas_call | solution.py:534
  43.0 1.7 %shard_map.113 = (f32[4,128,128]{2,1,0:T(8,128)}, f32[3,4]{1,0:T(4,128)}, f32[1,2]{1,0:T(1,128)}) custom-call(f32[4,128,128]{2,1,0:T(8,128)} %get-tuple-element.9.csd_in, f32[3,4]{1,0:T(4,128)} %get-tuple-element.10.stats_in, f32[1,2]{1,0:T(1,128)} %get-tuple-element.11.combined_in), custom_call_target="tpu_custom_call" | custom-call | tf_op jit(solution)/shard_map/pallas_call | solution.py:592

commit v3 on v2

--- a/solution.py
+++ b/solution.py
@@ -75,8 +75,8 @@
     dims,
     strain, final, func, mask, flags_in, window, ones, twist, twos,
     csd, stats, combined,
-    h, win, one, twi, two, fnat, mnat, rhs, y, lhs, xb, rb, pw, halo, ob, sums, rsums, gath, fg, re_c, flags,
-    load_sem, half_send, half_recv, x_send, x_recv, p_sem, s_sem, g_send, g_recv, o_sem, near_sem, far_sem,
+    h, win, one, twi, two, fnat, mnat, rhs, y, lhs, xb, rb, pw, halo, ob, sums, gath, fg, re_c, flags,
+    load_sem, half_send, half_recv, x_send, x_recv, p_sem, g_send, g_recv, o_sem, near_sem, far_sem, pair_sem,
 ):
     nx, nz, ny = dims
     total = nx * nz * ny
@@ -127,7 +127,6 @@
     for parity in range(2):
         for part in range(3):
             rhs[parity, pl.ds(KPAD * part + HALF, KPAD - HALF), :] = gap
-    sums[...] = jnp.zeros((16, 128), F32)
 
     pl.semaphore_wait(barrier, len(neighbours))
 
@@ -182,6 +181,7 @@
     def report_far():
         if two_away:
             pl.semaphore_wait(far_sem, len(two_away))
+        pl.semaphore_signal(pair_sem, inc=1, device_id=(me, 1 - det), device_id_type=MESH)
 
     def split(value):
         high = value.astype(BF16)
@@ -394,7 +394,7 @@
         mean_b = left(1) * weight_left + right(1) * weight_right
         filt = g_t / (mean_a * mean_b)
         sums[pl.ds(s, 1), :] = jnp.sum(filt * re_c[s], axis=0, keepdims=True)
-        sums[pl.ds(8 + s, 1), :] = jnp.sum(filt * f_t, axis=0, keepdims=True)
+        sums[pl.ds(SEG + s, 1), :] = jnp.sum(filt * f_t, axis=0, keepdims=True)
 
     def own(s):
         return lambda a: pw[s + 1, a]
@@ -408,96 +408,116 @@
     accumulate(SEG - 1, own(SEG - 2), lambda a: halo[a], ends, 1.0 - ends)
     accumulate(SEG - 2, own(SEG - 3), own(SEG - 1), 0.5, 0.5)
 
-    sum_copy = pltpu.make_async_remote_copy(
-        src_ref=sums, dst_ref=rsums, send_sem=s_sem.at[0], recv_sem=s_sem.at[1],
-        device_id=(me, 1 - det), device_id_type=MESH,
-    )
-    sum_copy.start()
+    pl.semaphore_wait(pair_sem, 1)
     lane = lax.broadcasted_iota(jnp.int32, (8, 128), 1)
     row = lax.broadcasted_iota(jnp.int32, (8, 128), 0)
-    quality = jnp.zeros((8, 128), F32)
+    whole = jnp.sum(sums[...], axis=1, keepdims=True)
+    message = jnp.sum(jnp.where(lane == row, jnp.broadcast_to(whole, (8, 128)), 0.0), axis=0, keepdims=True)
     for s in range(SEG):
-        quality = jnp.where(lane == s, flags[s].astype(F32), quality)
-    sum_copy.wait_recv()
-    whole = jnp.sum(sums[...] + rsums[...], axis=1, keepdims=True)
-
-    def to_lanes(column):
-        spread_out = jnp.where(lane == row, jnp.broadcast_to(column, (8, 128)), 0.0)
-        return jnp.broadcast_to(jnp.sum(spread_out, axis=0, keepdims=True), (8, 128))
-
-    numerator = to_lanes(whole[:8])
-    denominator = to_lanes(whole[8:])
+        message = jnp.where(lane[:1] == 2 * SEG + s, 0.5 * flags[s].astype(F32), message)
+
+    def row_copy(axis, mine, slot):
+        if axis == 0:
+            device = (y_peer(lax.rem(slot, ny)), slot // ny)
+        else:
+            device = (axes[axis][2](slot), det)
+        return pltpu.make_async_remote_copy(
+            src_ref=gath.at[axis, mine], dst_ref=gath.at[axis, mine],
+            send_sem=g_send.at[axis, slot], recv_sem=g_recv.at[axis, mine],
+            device_id=device, device_id_type=MESH,
+        )
+
+    def exchange(axis, count, mine, message, work):
+        gath[axis, mine] = message
+        for d in range(1, count):
+            row_copy(axis, mine, lax.rem(mine + d, count)).start()
+        for s in work:
+            finished(s)
+        for d in range(1, count):
+            slot = lax.rem(mine + d, count)
+            pltpu.make_async_remote_copy(
+                src_ref=gath.at[axis, slot], dst_ref=gath.at[axis, slot],
+                send_sem=g_send.at[axis, slot], recv_sem=g_recv.at[axis, slot],
+                device_id=(me, 1 - det), device_id_type=MESH,
+            ).wait_recv()
+
+    def rows_of(axis, start, count):
+        table = jnp.zeros((8, 128), F32)
+        for k in range(count):
+            table = jnp.where(row == k, jnp.broadcast_to(gath[axis, start + k], (8, 128)), table)
+        return table
+
+    def summed(x):
+        return jnp.sum(x, axis=0, keepdims=True)
+
+    def only(condition, x):
+        return jnp.where(condition, x, 0.0)
+
+    slot_y = det * ny + cy
+    exchange(0, 2 * ny, slot_y, message, (0, 1))
+    table = rows_of(0, 0, ny) + rows_of(0, ny, ny)
+    denominator = pltpu.roll(table, 128 - SEG, 1)
+    quality = pltpu.roll(table, 128 - 2 * SEG, 1)
     spread = jnp.sqrt(float(COARSE) / denominator)
-    estimate = float(np.sqrt(12.0 * COARSE)) * numerator / denominator
+    estimate = float(np.sqrt(12.0 * COARSE)) * table / denominator
     weight = quality / (spread * spread)
     per_spread = quality / spread
     up = quality * spread
-    inside = lane < SEG - 1
-    covariance = CORR * up * pltpu.roll(up, 127, 1)
-    pair_term = jnp.where(inside, CORR * per_spread * pltpu.roll(per_spread, 127, 1), 0.0)
-
-    rows = [weight, weight * estimate, pair_term, pltpu.roll(per_spread, SEG - 1, 1), per_spread, pltpu.roll(up, SEG - 1, 1)]
-    terms = jnp.zeros((8, 128), F32)
-    for i, value in enumerate(rows):
-        terms = jnp.where(row == i, value, terms)
-    terms = jnp.where((lane < SEG) & ((row < 3) | (lane == SEG - 1)), terms, 0.0)
-    next_first = jnp.zeros((8, 128), F32)
-    open_end = None
-
-    for axis, (count, mine, peer) in enumerate(axes):
-        gath[axis, mine] = terms
-
-        def gather_copy(d, axis=axis, count=count, mine=mine, peer=peer):
-            return pltpu.make_async_remote_copy(
-                src_ref=gath.at[axis, mine], dst_ref=gath.at[axis, mine],
-                send_sem=g_send.at[axis, d], recv_sem=g_recv.at[axis, mine],
-                device_id=(peer(lax.rem(mine + d, count)), det), device_id_type=MESH,
-            )
-
-        for d in range(1, count):
-            gather_copy(d).start()
-        for s in ((0, 1), (2, 3), ())[axis]:
-            finished(s)
-        for d in range(1, count):
-            source = lax.rem(mine + d, count)
-            pltpu.make_async_remote_copy(
-                src_ref=gath.at[axis, source], dst_ref=gath.at[axis, source],
-                send_sem=g_send.at[axis, d], recv_sem=g_recv.at[axis, source],
-                device_id=(peer(source), det), device_id_type=MESH,
-            ).wait_recv()
-        groups = [gath[axis, k] for k in range(count)]
-        total_terms, joints = groups[0], jnp.zeros((8, 128), F32)
-        for before, after in zip(groups[:-1], groups[1:]):
-            total_terms = total_terms + after
-            joints = joints + before * pltpu.roll(after, 1, 0)
-        total_terms = total_terms + jnp.where(row == 2, CORR * pltpu.roll(joints, 6, 0), 0.0)
-        terms = jnp.where(row < 3, total_terms, jnp.where(row == 4, groups[-1], groups[0]))
-        here = mine < count - 1
-        if open_end is not None:
-            here = jnp.logical_and(open_end, here)
-        next_first = jnp.where(here, gath[axis, jnp.minimum(mine + 1, count - 1)], next_first)
-        at_end = mine == count - 1
-        open_end = at_end if open_end is None else jnp.logical_and(open_end, at_end)
-
-    covariance = jnp.where(inside, covariance, CORR * up * pltpu.roll(next_first, 5, 0))
-    rows3 = jnp.where(row == 0, estimate, jnp.where(row == 1, spread, covariance))
-    stats[...] = rows3[:3, :SEG]
-
-    sweep = jnp.sum(terms, axis=1, keepdims=True)
-    weight_sum, weighted_sum, pair_sum = sweep[0:1], sweep[1:2], sweep[2:3]
+
+    def following_of(x):
+        return jnp.where(lane < SEG - 1, pltpu.roll(x, 127, 1), pltpu.roll(pltpu.roll(x, 7, 0), SEG - 1, 1))
+
+    valid = (lane < SEG) & (row < ny)
+    has_next = (lane < SEG - 1) | ((lane == SEG - 1) & (row < ny - 1))
+    pair_term = only(valid & has_next, CORR * per_spread * following_of(per_spread))
+    covariance = only(has_next, CORR * up * following_of(up))
+    own_row = row == cy
+    estimate_own = summed(only(own_row, estimate))
+    spread_own = summed(only(own_row, spread))
+    covariance_own = summed(only(own_row, covariance))
+    up_own = summed(only(own_row, up))
+
+    message = summed(
+        only(valid, weight)
+        + pltpu.roll(only(valid, weight * estimate), 4, 1)
+        + pltpu.roll(pair_term, 8, 1)
+        + only((row == 0) & (lane == 12), pltpu.roll(per_spread, 12, 1))
+        + only((row == 0) & (lane == 13), pltpu.roll(up, 13, 1))
+        + only((row == ny - 1) & (lane == 14), pltpu.roll(per_spread, 15 - SEG, 1))
+    )
+    at_end = cy == ny - 1
+    next_first = jnp.zeros((1, 128), F32)
+    for axis, work in ((1, (2, 3)), (2, ())):
+        count, mine, _ = axes[axis]
+        exchange(axis, count, mine, message, work)
+        table = rows_of(axis, 0, count)
+        found = (row == mine + 1) & (row < count) & (lane == 13) & at_end
+        next_first = next_first + summed(only(found, table))
+        at_end = jnp.logical_and(at_end, mine == count - 1)
+        joint = CORR * table * pltpu.roll(pltpu.roll(table, 7, 0), 2, 1)
+        message = summed(
+            only((lane < 12) | ((row == 0) & (lane < 14)) | ((row == count - 1) & (lane == 14)), table)
+            + only((lane == 8) & (row < count - 1), pltpu.roll(joint, 122, 1))
+        )
+
+    last_lane = lane[:1] == SEG - 1
+    covariance_own = covariance_own + only(last_lane, CORR * up_own * pltpu.roll(next_first, 115 + SEG - 1, 1))
+    three = jnp.where(row == 0, estimate_own, jnp.where(row == 1, spread_own, covariance_own))
+    stats[...] = three[:3, :SEG]
+
+    def lanes_from(at):
+        return jnp.sum(only((lane[:1] >= at) & (lane[:1] < at + 4), message), axis=1, keepdims=True)
+
+    weight_sum, weighted_sum, pair_sum = lanes_from(0), lanes_from(4), lanes_from(8)
     root = float(np.sqrt(SEG * total))
     pick = lax.broadcasted_iota(jnp.int32, (1, 2), 1)
     combined[...] = jnp.where(
         pick == 0, root * (weighted_sum / weight_sum), root * (jnp.sqrt(weight_sum + 2.0 * pair_sum) / weight_sum)
     )
 
-    for axis, (count, mine, peer) in enumerate(axes):
+    for axis, count, mine in ((0, 2 * ny, slot_y), (1, nz, cz), (2, nx, cx)):
         for d in range(1, count):
-            pltpu.make_async_remote_copy(
-                src_ref=gath.at[axis, mine], dst_ref=gath.at[axis, mine],
-                send_sem=g_send.at[axis, d], recv_sem=g_recv.at[axis, mine],
-                device_id=(peer(lax.rem(mine + d, count)), det), device_id_type=MESH,
-            ).wait_send()
+            row_copy(axis, mine, lax.rem(mine + d, count)).wait_send()
 
     for end in range(2):
 
@@ -512,7 +532,6 @@
     for s in range(-1, SEG):
         for pair in range(2):
             x_copy(s, pair).wait_send()
-    sum_copy.wait_send()
 
 
 def writer(csd_in, stats_in, combined_in, csd, stats, combined, csd_v, stats_v, combined_v, sems):
@@ -556,9 +575,8 @@
             pltpu.VMEM((SEG + 1, 2, 64, 128), F32),
             pltpu.VMEM((2, 64, 128), F32),
             pltpu.VMEM((SEG, 128, 128), F32),
-            pltpu.VMEM((16, 128), F32),
-            pltpu.VMEM((16, 128), F32),
-            pltpu.VMEM((3, 8, 8, 128), F32),
+            pltpu.VMEM((8, 128), F32),
+            pltpu.VMEM((3, 16, 1, 128), F32),
             pltpu.VMEM((128, 128), F32),
             pltpu.VMEM((SEG, 64, 128), F32),
             pltpu.SMEM((SEG,), jnp.int32),
@@ -568,10 +586,10 @@
             dma((SEG + 1, 2)),
             dma((SEG + 1, 2)),
             dma((2,)),
-            dma((2,)),
-            dma((3, 8)),
-            dma((3, 8)),
+            dma((3, 16)),
+            dma((3, 16)),
             dma((SEG + 1,)),
+            pltpu.SemaphoreType.REGULAR,
             pltpu.SemaphoreType.REGULAR,
             pltpu.SemaphoreType.REGULAR,
         ],

time: 44.8 us -> 44 us (0.982)
  Pallas kernels: 44.1 us -> 43.2 us
    pallas_call x1, Pallas kernels: 42.3 us -> 41.5 us  [on_device(): pl.pallas_call(functools.partial(kernel, dims), out_shape=(jax.ShapeDtype...]
where the time goes in v3:
time: 44 us; the launch traced here: 43.9 us
  Pallas kernels  43.2 us (98%)
  between operations  0.64 us (1%)
    pallas_call x1, Pallas kernels, on_device(): pl.pallas_call(functools.partial(kernel, dims), out_shape=(jax.ShapeDtype...  41.5 us
    pallas_call x1, Pallas kernels, on_device(): pl.pallas_call(writer, out_shape=(jax.ShapeDtypeStruct((SEG, 128, 128), F...  1.71 us

profile of v3, /device:TPU:8, one launch (start us, length us, event | category | flops | bytes accessed | tf_op | source)
XLA Modules:
  0.0 43.9 jit_solution(11029476424091047548)
XLA Ops:
  0.6 41.5 %shard_map.112 = (f32[4,128,128]{2,1,0:T(8,128)}, f32[3,4]{1,0:T(4,128)}, f32[1,2]{1,0:T(1,128)}) custom-call(f32[1,4,192,512]{3,2,1,0:T(8,128)} %strain.1, f32[1,192,512]{2,1,0:T(8,128)} %final.1, f32[64,128]{1,0:T(8,128)} %bitcast.8, s32[64,128]{1,0:T(8,128)} %bitcast.9, s32[4]{0:T(128)} %flags_in.1, f32[192,512]{1,0:T(8,128)} %constant.8.clone.window, ...), custom_call_target="tpu_custom_call" | custom-call | tf_op jit(solution)/shard_map/pallas_call | solution.py:553
  42.2 1.7 %shard_map.113 = (f32[4,128,128]{2,1,0:T(8,128)}, f32[3,4]{1,0:T(4,128)}, f32[1,2]{1,0:T(1,128)}) custom-call(f32[4,128,128]{2,1,0:T(8,128)} %get-tuple-element.9.csd_in, f32[3,4]{1,0:T(4,128)} %get-tuple-element.10.stats_in, f32[1,2]{1,0:T(1,128)} %get-tuple-element.11.combined_in), custom_call_target="tpu_custom_call" | custom-call | tf_op jit(solution)/shard_map/pallas_call | solution.py:610

commit v4 on v3

--- a/solution.py
+++ b/solution.py
@@ -48,7 +48,7 @@
         ones.append(np.pad(one, ((0, 0), (0, KPAD - HALF))))
         turn = 2.0 * np.pi * (bins[:, None] * col[None, :] % LENGTH) / LENGTH
         twists.append(np.stack([np.cos(turn), np.sin(turn)]))
-    one_hi, one_lo = split_np(np.concatenate(ones))
+    stacked = [part for one in ones for part in split_np(one)]
 
     twos = []
     t = np.arange(32)
@@ -65,7 +65,7 @@
     two_hi, two_lo = split_np(np.stack(twos) * (8.0 / (3.0 * LENGTH) / BIN) ** 0.5)
     return (
         window.astype(np.float32),
-        np.stack([one_hi, one_lo]),
+        np.concatenate(stacked),
         np.concatenate(twists, axis=1).astype(np.float32),
         np.stack([two_hi, two_lo], axis=1),
     )
@@ -117,16 +117,16 @@
 
     outgoing = [load(strain.at[0, s], h.at[s + 1]) for s in (0, SEG - 1)]
     early = [load(window, win), load(strain.at[0, 1], h.at[2])]
-    early += [load(ones.at[part % 2], one.at[:, pl.ds(KPAD * part, KPAD)]) for part in range(3)]
+    early.append(load(ones, one))
     twist_load = load(twist, twi)
-    two_loads = [load(twos.at[:, (0, 0, 1)[part]], two.at[:, pl.ds(256 * part, 256)]) for part in range(3)]
+    two_loads = [load(twos, two)]
     late = [load(strain.at[0, s], h.at[s + 1]) for s in range(2, SEG - 1)]
     late += [load(func, fnat), load(mask, mnat), load(flags_in, flags)]
 
     gap = jnp.zeros((KPAD - HALF, COLS), BF16)
     for parity in range(2):
-        for part in range(3):
-            rhs[parity, pl.ds(KPAD * part + HALF, KPAD - HALF), :] = gap
+        for part in range(2):
+            rhs[parity, part, HALF:, :] = gap
 
     pl.semaphore_wait(barrier, len(neighbours))
 
@@ -187,6 +187,11 @@
         high = value.astype(BF16)
         return high, (value - high.astype(F32)).astype(BF16)
 
+    def passes(left, right_high, right_low, count):
+        both = jnp.dot(left, right_high, preferred_element_type=F32)
+        rest = jnp.dot(left[:count], right_low, preferred_element_type=F32)
+        return both[:count] + (both[count:] + rest)
+
     def first_stage(s, p, slot=0, end=None):
         cols = pl.ds(256 * p, 256)
         if end is not None:
@@ -208,15 +213,15 @@
             w = win[rows, cols]
             for parity, value in ((0, lower + w * (upper - lower)), (1, w * (upper + lower) - lower)):
                 high, low = split(value)
-                rhs[parity, rows, cols] = high
-                rhs[parity, pl.ds(KPAD + 16 * i, 16), cols] = high
-                rhs[parity, pl.ds(2 * KPAD + 16 * i, 16), cols] = low
+                rhs[parity, 0, rows, cols] = high
+                rhs[parity, 1, rows, cols] = low
             return carry
 
         for i in range(HALF // 16):
             windowed(i, 0)
-        y[slot, : 2 * EVEN, cols] = jnp.dot(one[: 2 * EVEN], rhs[0, :, cols], preferred_element_type=F32)
-        y[slot, 2 * EVEN :, cols] = jnp.dot(one[2 * EVEN :], rhs[1, :, cols], preferred_element_type=F32)
+        for parity, at, count in ((0, 0, 2 * EVEN), (1, 2 * EVEN, 2 * ODD)):
+            left = one[2 * at : 2 * at + 2 * count]
+            y[slot, at : at + count, cols] = passes(left, rhs[parity, 0, :, cols], rhs[parity, 1, :, cols], count)
 
     def second_stage(s, slot=0):
         def turned(real_at, imag_at, i):
@@ -236,8 +241,7 @@
                 for at, z in zip((0, 128), pair):
                     high, low = split(z)
                     lhs[q, rows, pl.ds(at, 128)] = high
-                    lhs[q, rows, pl.ds(256 + at, 128)] = low
-                    lhs[q, rows, pl.ds(512 + at, 128)] = high
+                    lhs[q, pl.ds(ROWS + 16 * i, 16), pl.ds(at, 128)] = low
 
         def turned_even(i, carry):
             turned(0, EVEN, i)
@@ -249,11 +253,11 @@
 
         for i in range(ROWS // 16):
             (turned_even if i < EVEN // 16 else turned_odd)(i, 0)
+        for q in range(4):
+            out = passes(lhs[q], two[q, 0], two[q, 1], ROWS)
+            xb[s + 1, 0, q] = out[:, :128]
+            xb[s + 1, 1, q] = out[:, 128:]
         for pair in range(2):
-            for q in (2 * pair, 2 * pair + 1):
-                out = jnp.dot(lhs[q], two[q], preferred_element_type=F32)
-                xb[s + 1, 0, q] = out[:, :128]
-                xb[s + 1, 1, q] = out[:, 128:]
             x_copy(s, pair).start()
 
     def x_copy(s, pair):
@@ -535,13 +539,17 @@
 
 
 def writer(csd_in, stats_in, combined_in, csd, stats, combined, csd_v, stats_v, combined_v, sems):
-    held = (csd_v, stats_v, combined_v)
-    for way, pairs in enumerate((zip((csd_in, stats_in, combined_in), held), zip(held, (csd, stats, combined)))):
-        copies = [pltpu.make_async_copy(src, dst, sems.at[way, i]) for i, (src, dst) in enumerate(pairs)]
-        for copy in copies:
-            copy.start()
-        for copy in copies:
-            copy.wait()
+    parts = [(csd_in.at[s], csd_v.at[s], csd.at[s]) for s in range(SEG)]
+    parts += [(stats_in, stats_v, stats), (combined_in, combined_v, combined)]
+    reads = [pltpu.make_async_copy(src, held, sems.at[0, i]) for i, (src, held, _) in enumerate(parts)]
+    writes = [pltpu.make_async_copy(held, dst, sems.at[1, i]) for i, (_, held, dst) in enumerate(parts)]
+    for read in reads:
+        read.start()
+    for read, write in zip(reads, writes):
+        read.wait()
+        write.start()
+    for write in writes:
+        write.wait()
 
 
 def on_device(dims, strain, final_half, intersection_function, notch_mask, quality_flags):
@@ -562,14 +570,14 @@
         scratch_shapes=[
             pltpu.VMEM((SEG + 2, HALF, COLS), F32),
             pltpu.VMEM((HALF, COLS), F32),
-            pltpu.VMEM((2 * ROWS, 3 * KPAD), BF16),
+            pltpu.VMEM((4 * ROWS, KPAD), BF16),
             pltpu.VMEM((2, ROWS, COLS), F32),
-            pltpu.VMEM((4, 3 * 256, 256), BF16),
+            pltpu.VMEM((4, 2, 256, 256), BF16),
             pltpu.VMEM((64, 128), F32),
             pltpu.VMEM((64, 128), jnp.int32),
-            pltpu.VMEM((2, 3 * KPAD, COLS), BF16),
+            pltpu.VMEM((2, 2, KPAD, COLS), BF16),
             pltpu.VMEM((3, 2 * ROWS, COLS), F32),
-            pltpu.VMEM((4, ROWS, 3 * 256), BF16),
+            pltpu.VMEM((4, 2 * ROWS, 256), BF16),
             pltpu.VMEM((SEG + 1, 2, 4, ROWS, 128), F32),
             pltpu.VMEM((SEG + 1, 4, ROWS, 128), F32),
             pltpu.VMEM((SEG + 1, 2, 64, 128), F32),
@@ -620,7 +628,7 @@
             pltpu.VMEM((SEG, 128, 128), F32),
             pltpu.VMEM((3, SEG), F32),
             pltpu.VMEM((1, 2), F32),
-            dma((2, 3)),
+            dma((2, SEG + 2)),
         ],
     )(csd, stats, combined)
     csd = csd.reshape(SEG, 64, 2, 128).transpose(0, 2, 1, 3).reshape(SEG, 2, 64 * 128)

time: 44 us -> 44 us (level)
  no operation moved by 1% of the time
where the time goes in v4:
time: 44 us; the launch traced here: 43.9 us
  Pallas kernels  43.2 us (98%)
  between operations  0.64 us (1%)
    pallas_call x1, Pallas kernels, on_device(): pl.pallas_call(functools.partial(kernel, dims), out_shape=(jax.ShapeDtype...  41.6 us
    pallas_call x1, Pallas kernels, on_device(): pl.pallas_call(writer, out_shape=(jax.ShapeDtypeStruct((SEG, 128, 128), F...  1.67 us

profile of v4, /device:TPU:8, one launch (start us, length us, event | category | flops | bytes accessed | tf_op | source)
XLA Modules:
  0.0 43.9 jit_solution(6882777719095516186)
XLA Ops:
  0.6 41.6 %shard_map.112 = (f32[4,128,128]{2,1,0:T(8,128)}, f32[3,4]{1,0:T(4,128)}, f32[1,2]{1,0:T(1,128)}) custom-call(f32[1,4,192,512]{3,2,1,0:T(8,128)} %strain.1, f32[1,192,512]{2,1,0:T(8,128)} %final.1, f32[64,128]{1,0:T(8,128)} %bitcast.8, s32[64,128]{1,0:T(8,128)} %bitcast.9, s32[4]{0:T(128)} %flags_in.1, f32[192,512]{1,0:T(8,128)} %constant.8.clone.window, ...), custom_call_target="tpu_custom_call" | custom-call | tf_op jit(solution)/shard_map/pallas_call | solution.py:561
  42.2 1.7 %shard_map.113 = (f32[4,128,128]{2,1,0:T(8,128)}, f32[3,4]{1,0:T(4,128)}, f32[1,2]{1,0:T(1,128)}) custom-call(f32[4,128,128]{2,1,0:T(8,128)} %get-tuple-element.9.csd_in, f32[3,4]{1,0:T(4,128)} %get-tuple-element.10.stats_in, f32[1,2]{1,0:T(1,128)} %get-tuple-element.11.combined_in), custom_call_target="tpu_custom_call" | custom-call | tf_op jit(solution)/shard_map/pallas_call | solution.py:618
